TPU v7x, 32 devices: a whole 2x2x4 slice. The times are simulated.
32 devices in a mesh: gx: 4 (over y, x), gy: 4 (over z), layer: 2 (over core).
Axes of the slice: x: 2, y: 2, z: 4, core: 2. Of those that a mesh axis runs over, the one named last changes fastest.
Arguments:
- profiles: bfloat16 [2, 4, 65536, 256], P('layer', 'gx', 'gy'), may hold values from 0.049804688 to 2
- time_weight: bfloat16 [256], replicated, may hold values from 0 to 0.029907227
- slot_cell: int32 [2, 4, 65536], P('layer', 'gx', 'gy'), may hold values from 0 to 65535
- inst_count: int32 [2, 4, 4], P('layer', 'gx', 'gy'), may hold values from 1 to 16384, as said below
- metal: float32 [6, 512, 2048], P('layer', 'gx', 'gy'), may hold values from 0.5 to 4
- via_density: float32 [512, 2048], P('gx', 'gy'), may hold values from 0.5 to 4
- pad: float32 [512, 2048], P('gx', 'gy'), may hold values from 0.05 to 0.5
- start_drop: float32 [6, 512, 2048], P('layer', 'gx', 'gy'), may hold values from 0 to 1
Outputs:
- drop: float32 [6, 512, 2048], P('layer', 'gx', 'gy')
- residual: float32 [6, 512, 2048], P('layer', 'gx', 'gy')
Inputs may be any that keep to these rules, and one draw needn't show every extreme that they name: The first inst_count slots of a device are live, the rest are padding; and one device is full in every draw. `slot_cell`: row-major cell index within the tile of 128 x 512 cells.
All inputs are finite; a program needn't handle non-finite values.
Results may differ from a plain program's by a relative error of at most 0.0018.
Values sent between devices are 32-bit elements; how exact they have to be, the bound alone decides.
A program may use at most 64 MiB of HBM per device.

v0:
```python
import jax
import jax.numpy as jnp
from jax import lax
from jax.sharding import PartitionSpec as P

BLOCK = 512
ITERS = 3


def from_behind(value, axis, steps):
    count = lax.axis_size(axis)
    first, last = (max(0, -steps), min(count, count - steps))
    return lax.ppermute(value, axis, [(source, source + steps) for source in range(first, last)])


def with_halo(shard, sides, width):
    for axis, dim in sides:
        devices, length = (lax.axis_size(axis), shard.shape[dim])
        up = [(i, (i + 1) % devices) for i in range(devices - 1)]
        down = [(j, i) for i, j in up]
        last = lax.slice_in_dim(shard, length - width, length, axis=dim)
        first = lax.slice_in_dim(shard, 0, width, axis=dim)
        before = lax.ppermute(last, axis, up)
        after = lax.ppermute(first, axis, down)
        shard = jnp.concatenate([before, shard, after], axis=dim)
    return shard


def harmonic(values, beside):
    return 2.0 * values * beside / (values + beside)


def links(extended, via_column):
    middle = extended[1:-1, 1:-1, 1:-1]
    east_link = harmonic(middle, extended[1:-1, 2:, 1:-1])
    west_link = harmonic(middle, extended[1:-1, :-2, 1:-1])
    north_link = harmonic(middle, extended[1:-1, 1:-1, 2:])
    south_link = harmonic(middle, extended[1:-1, 1:-1, :-2])
    upper_link = via_column * harmonic(middle, extended[2:, 1:-1, 1:-1])
    lower_link = via_column * harmonic(middle, extended[:-2, 1:-1, 1:-1])
    return (east_link, west_link, north_link, south_link, upper_link, lower_link)


def diagonal_of(conduct):
    east_link, west_link, north_link, south_link, upper_link, lower_link = conduct
    return east_link + west_link + north_link + south_link + upper_link + lower_link


def operate(field, extended, conduct, diagonal):
    east_link, west_link, north_link, south_link, upper_link, lower_link = conduct
    result = (
        diagonal * field
        - east_link * extended[1:-1, 2:, 1:-1]
        - west_link * extended[1:-1, :-2, 1:-1]
    )
    result = result - north_link * extended[1:-1, 1:-1, 2:] - south_link * extended[1:-1, 1:-1, :-2]
    return result - upper_link * extended[2:, 1:-1, 1:-1] - lower_link * extended[:-2, 1:-1, 1:-1]


def both_sums(residual, scaled, image):
    return lax.psum((jnp.sum(residual * scaled), jnp.sum(scaled * image)), ("gx", "gy", "layer"))


def solve(apply, diagonal, rhs, start):
    solution = start
    residual = rhs - apply(start)
    scaled = residual / diagonal
    image = apply(scaled)
    energy, curvature = both_sums(residual, scaled, image)
    step_size = energy / curvature
    direction, along = (scaled, image)
    for iteration in range(ITERS):
        solution = solution + step_size * direction
        residual = residual - step_size * along
        if iteration + 1 < ITERS:
            scaled = residual / diagonal
            image = apply(scaled)
            energy_next, curvature = both_sums(residual, scaled, image)
            momentum = energy_next / energy
            step_size = energy_next / (curvature - momentum * energy_next / step_size)
            direction = scaled + momentum * direction
            along = image + momentum * along
            energy = energy_next
    return (solution, residual)


def per_device(profiles, time_weight, slot_cell, inst_count, metal, via_density, pad, start_drop):
    tile_rows, tile_cols = (metal.shape[1], metal.shape[2])
    slot_current = jnp.dot(
        profiles.reshape(-1, profiles.shape[-1]), time_weight, preferred_element_type=jnp.float32
    )
    slot_cells = slot_cell.reshape(-1)
    live_count = inst_count.reshape(())
    positions = jnp.arange(slot_cells.shape[0], dtype=jnp.int32)
    slot_current = jnp.where(positions < live_count, slot_current, 0.0)
    block_rows = min(BLOCK, slot_cells.shape[0])
    blocks_live = (live_count + block_rows - 1) // block_rows
    row_ids = jnp.arange(tile_rows, dtype=jnp.int32)
    col_ids = jnp.arange(tile_cols, dtype=jnp.int32)

    def add_block(block_index, total):
        first = block_index * block_rows
        cells = lax.dynamic_slice_in_dim(slot_cells, first, block_rows)
        amounts = lax.dynamic_slice_in_dim(slot_current, first, block_rows)
        left = jnp.where(cells[:, None] // tile_cols == row_ids[None, :], amounts[:, None], 0.0)
        left_high = left.astype(jnp.bfloat16)
        left_low = (left - left_high.astype(jnp.float32)).astype(jnp.bfloat16)
        right = (cells[:, None] % tile_cols == col_ids[None, :]).astype(jnp.bfloat16)
        dims = (((0,), (0,)), ((), ()))
        upper_part = lax.dot_general(left_high, right, dims, preferred_element_type=jnp.float32)
        lower_part = lax.dot_general(left_low, right, dims, preferred_element_type=jnp.float32)
        return total + (upper_part + lower_part)

    partial_value = lax.fori_loop(
        0, blocks_live, add_block, jnp.zeros((tile_rows, tile_cols), jnp.float32)
    )
    others = from_behind(partial_value, "layer", -1)
    bottom = lax.axis_index("layer") == 0
    current = jnp.where(bottom, partial_value + others, 0.0)
    rhs = jnp.zeros_like(metal).at[0].set(current)
    extended = with_halo(metal, (("gx", 1), ("gy", 2), ("layer", 0)), 1)
    conduct = links(extended, via_density[None])
    top = lax.axis_index("layer") == lax.axis_size("layer") - 1
    diagonal = diagonal_of(conduct).at[-1].add(jnp.where(top, pad, 0.0))

    def apply(field):
        rims = with_halo(field, (("gx", 1), ("gy", 2), ("layer", 0)), 1)
        return operate(field, rims, conduct, diagonal)

    solution, residual = solve(apply, diagonal, rhs, start_drop)
    return (solution, residual)


def solution(mesh):
    in_specs = (
        P("layer", "gx", "gy", None),
        P(),
        P("layer", "gx", "gy"),
        P("layer", "gx", "gy"),
        P("layer", "gx", "gy"),
        P("gx", "gy"),
        P("gx", "gy"),
        P("layer", "gx", "gy"),
    )
    out_specs = (P("layer", "gx", "gy"), P("layer", "gx", "gy"))
    return jax.shard_map(
        per_device, mesh=mesh, in_specs=in_specs, out_specs=out_specs, check_vma=False
    )
```

profile of v0, /device:TPU:0, one launch (start us, length us, event | category | flops | bytes accessed | tf_op | source)
XLA Modules:
  0.0 358.4 jit_solution(6183316675431380486)
XLA Ops:
  1.5 4.9 %collective-permute-start.2 = (f32[3,1,512]{2,1,0:T(1,128)S(1)}, f32[3,1,512]{2,1,0:T(1,128)S(1)}, u32[]{:S(2)}, u32[]{:S(2)}) collective-permute-start(f32[3,1,512]{2,1,0:T(1,128)S(1)} %get-tuple-element.200), channel_id=1, source_target_pairs={{0,8},{8,16},{16,24},{1,9},{9,17},{17,25},{2,10},{10,18},{18,26},{... | collective-permute-start | bytes 18440 | tf_op jit(solution)/shard_map/ppermute | solution.py:23
  8.5 4.5 %collective-permute-start.8 = (f32[3,1,512]{2,1,0:T(1,128)S(1)}, f32[3,1,512]{2,1,0:T(1,128)S(1)}, u32[]{:S(2)}, u32[]{:S(2)}) collective-permute-start(f32[3,1,512]{2,1,0:T(1,128)S(1)} %get-tuple-element.198), channel_id=1, source_target_pairs={{0,8},{8,16},{16,24},{1,9},{9,17},{17,25},{2,10},{10,18},{18,26},{... | collective-permute-start | bytes 18440 | tf_op jit(solution)/shard_map/ppermute | solution.py:23
  15.7 5.8 %fusion.19 = f32[1,16384]{1,0:T(1,128)S(1)} fusion(bf16[256,1]{0,1:T(2,128)(2,1)S(1)} %reshape.111, bf16[1,1,16384,256]{3,2,1,0:T(8,128)(2,1)} %param.14), kind=kOutput, calls=%fused_computation.28 | convolution fusion | flops 8388608 | bytes 8454656 | tf_op jit(solution)/shard_map/dot_general | solution.py:89
  21.5 12.7 %while.15 = (s32[]{:T(128)}, f32[128,512]{1,0:T(8,128)S(1)}, s32[]{:T(128)}, s32[16384]{0:T(1024)}, f32[16384]{0:T(1024)S(1)}, /*index=5*/s32[]{:T(128)}, s32[]{:T(128)}, s32[]{:T(128)}, s32[]{:T(128)}) while((s32[]{:T(128)}, f32[128,512]{1,0:T(8,128)S(1)}, s32[]{:T(128)}, s32[16384]{0:T(1024)}, f32[16384]{0:T(1024)S(1)}, ...), condition=%wide.region_1.2_spmd.clone, body=%wide.region_0.1_spmd.clone.sunk | while | flops 135407104 | bytes 1071251 | solution.py:114
  35.7 22.6 %collective-permute-start.4 = (f32[3,130,1]{2,1,0:T(8,128)S(1)}, f32[3,130,1]{2,1,0:T(8,128)S(1)}, u32[]{:S(2)}, u32[]{:S(2)}) collective-permute-start(f32[3,130,1]{2,1,0:T(8,128)S(1)} %get-tuple-element.190), channel_id=1, source_target_pairs={{0,2},{2,4},{4,6},{1,3},{3,5},{5,7},{8,10},{10,12},{12,14},{9,11},... | collective-permute-start | bytes 4688 | tf_op jit(solution)/shard_map/ppermute | solution.py:23
  59.8 21.1 %collective-permute-start.10 = (f32[3,130,1]{2,1,0:T(8,128)S(1)}, f32[3,130,1]{2,1,0:T(8,128)S(1)}, u32[]{:S(2)}, u32[]{:S(2)}) collective-permute-start(f32[3,130,1]{2,1,0:T(8,128)S(1)} %get-tuple-element.188), channel_id=1, source_target_pairs={{0,2},{2,4},{4,6},{1,3},{3,5},{5,7},{8,10},{10,12},{12,14},{9,11},... | collective-permute-start | bytes 4688 | tf_op jit(solution)/shard_map/ppermute | solution.py:23
  88.3 21.1 %collective-permute-done.9 = f32[3,130,1]{2,1,0:T(8,128)S(1)} collective-permute-done((f32[3,130,1]{2,1,0:T(8,128)S(1)}, f32[3,130,1]{2,1,0:T(8,128)S(1)}, u32[]{:S(2)}, u32[]{:S(2)}) %collective-permute-start.9) | collective-permute-done | bytes 1592 | tf_op jit(solution)/shard_map/ppermute | solution.py:24
  117.8 3.7 %fusion.83 = (f32[3,128,512]{2,1,0:T(8,128)S(1)}, f32[3,128,512]{2,1,0:T(8,128)S(1)}) fusion(f32[3,128,512]{2,1,0:T(8,128)S(1)} %fusion.76, f32[3,128,512]{2,1,0:T(8,128)S(1)} %get-tuple-element.169, f32[3,130,1]{2,1,0:T(8,128)S(1)} %collective-permute-done.9, f32[3,1,512]{2,1,0:T(1,128)S(1)} %collective-permute-done.7, f32[3,128,512]{2,1,0:T(8,128)S(1)} %copy-done.6, ...), kind=kLoop, calls=%fused_computation.238 | loop fusion | flops 10616832 | bytes 6332544 | tf_op jit(solution)/shard_map/div | solution.py:67
  124.2 8.7 %collective-permute-done.13 = f32[3,1,512]{2,1,0:T(1,128)S(1)} collective-permute-done((f32[3,1,512]{2,1,0:T(1,128)S(1)}, f32[3,1,512]{2,1,0:T(1,128)S(1)}, u32[]{:S(2)}, u32[]{:S(2)}) %collective-permute-start.13) | collective-permute-done | bytes 6176 | tf_op jit(solution)/shard_map/ppermute | solution.py:24
  133.1 3.7 %collective-permute-start.16 = (f32[3,130,1]{2,1,0:T(8,128)S(1)}, f32[3,130,1]{2,1,0:T(8,128)S(1)}, u32[]{:S(2)}, u32[]{:S(2)}) collective-permute-start(f32[3,130,1]{2,1,0:T(8,128)S(1)} %get-tuple-element.186), channel_id=1, source_target_pairs={{0,2},{2,4},{4,6},{1,3},{3,5},{5,7},{8,10},{10,12},{12,14},{9,11},... | collective-permute-start | bytes 4688 | tf_op jit(solution)/shard_map/ppermute | solution.py:23
  140.6 4.1 %collective-permute-done.15 = f32[3,130,1]{2,1,0:T(8,128)S(1)} collective-permute-done((f32[3,130,1]{2,1,0:T(8,128)S(1)}, f32[3,130,1]{2,1,0:T(8,128)S(1)}, u32[]{:S(2)}, u32[]{:S(2)}) %collective-permute-start.15) | collective-permute-done | bytes 1592 | tf_op jit(solution)/shard_map/ppermute | solution.py:24
  150.7 5.0 %multiply_reduce_fusion.4 = (f32[]{:T(128)}, f32[]{:T(128)}, f32[3,128,512]{2,1,0:T(8,128)}) fusion(f32[3,128,512]{2,1,0:T(8,128)S(1)} %get-tuple-element.165, f32[3,128,512]{2,1,0:T(8,128)S(1)} %get-tuple-element.166, f32[3,128,512]{2,1,0:T(8,128)S(1)} %get-tuple-element.169, f32[3,130,1]{2,1,0:T(8,128)S(1)} %collective-permute-done.15, ...), kind=kLoop, calls=%fused_computation.184 | loop fusion | flops 11010046 | bytes 6070408 | tf_op jit(solution)/shard_map/reduce_sum | solution.py:61
  155.7 40.6 %all-reduce.3 = (f32[]{:T(128)}, f32[]{:T(128)}) all-reduce(f32[]{:T(128)} %get-tuple-element.141, f32[]{:T(128)} %get-tuple-element.140), channel_id=1, replica_groups=mesh['gx'=4,'gy'=4,'layer'=2] {'gx','gy','layer'}, use_global_device_ids=true, to_apply=%region_3.4 | all-reduce | flops 2 | bytes 16 | tf_op jit(solution)/shard_map/psum | solution.py:61
  199.3 4.2 %collective-permute-start.20 = (f32[3,1,512]{2,1,0:T(1,128)S(1)}, f32[3,1,512]{2,1,0:T(1,128)S(1)}, u32[]{:S(2)}, u32[]{:S(2)}) collective-permute-start(f32[3,1,512]{2,1,0:T(1,128)S(1)} %get-tuple-element.194), channel_id=1, source_target_pairs={{0,8},{8,16},{16,24},{1,9},{9,17},{17,25},{2,10},{10,18},{18,26},{... | collective-permute-start | bytes 18440 | tf_op jit(solution)/shard_map/ppermute | solution.py:23
  204.9 4.2 %collective-permute-done.19 = f32[3,1,512]{2,1,0:T(1,128)S(1)} collective-permute-done((f32[3,1,512]{2,1,0:T(1,128)S(1)}, f32[3,1,512]{2,1,0:T(1,128)S(1)}, u32[]{:S(2)}, u32[]{:S(2)}) %collective-permute-start.19) | collective-permute-done | bytes 6176 | tf_op jit(solution)/shard_map/ppermute | solution.py:24
  214.7 4.4 %collective-permute-done.21 = f32[3,130,1]{2,1,0:T(8,128)S(1)} collective-permute-done((f32[3,130,1]{2,1,0:T(8,128)S(1)}, f32[3,130,1]{2,1,0:T(8,128)S(1)}, u32[]{:S(2)}, u32[]{:S(2)}) %collective-permute-start.21) | collective-permute-done | bytes 1592 | tf_op jit(solution)/shard_map/ppermute | solution.py:24
  225.2 6.3 %multiply_reduce_fusion.2 = (f32[]{:T(128)}, f32[]{:T(128)}, f32[3,128,512]{2,1,0:T(8,128)}) fusion(f32[3,128,512]{2,1,0:T(8,128)S(1)} %get-tuple-element.162, f32[3,128,512]{2,1,0:T(8,128)S(1)} %get-tuple-element.163, f32[3,128,512]{2,1,0:T(8,128)} %copy-done.4, f32[3,130,1]{2,1,0:T(8,128)S(1)} %collective-permute-done.21, ...), kind=kLoop, calls=%fused_computation.181 | loop fusion | flops 11010046 | bytes 6070408 | tf_op jit(solution)/shard_map/reduce_sum | solution.py:61
  231.5 39.9 %all-reduce.2 = (f32[]{:T(128)}, f32[]{:T(128)}) all-reduce(f32[]{:T(128)} %get-tuple-element.139, f32[]{:T(128)} %get-tuple-element.138), channel_id=1, replica_groups=mesh['gx'=4,'gy'=4,'layer'=2] {'gx','gy','layer'}, use_global_device_ids=true, to_apply=%region_7.8 | all-reduce | flops 2 | bytes 16 | tf_op jit(solution)/shard_map/psum | solution.py:61
  278.0 4.2 %collective-permute-start.26 = (f32[3,1,512]{2,1,0:T(1,128)S(1)}, f32[3,1,512]{2,1,0:T(1,128)S(1)}, u32[]{:S(2)}, u32[]{:S(2)}) collective-permute-start(f32[3,1,512]{2,1,0:T(1,128)S(1)} %get-tuple-element.192), channel_id=1, source_target_pairs={{0,8},{8,16},{16,24},{1,9},{9,17},{17,25},{2,10},{10,18},{18,26},{... | collective-permute-start | bytes 18440 | tf_op jit(solution)/shard_map/ppermute | solution.py:23
  283.6 4.2 %collective-permute-done.25 = f32[3,1,512]{2,1,0:T(1,128)S(1)} collective-permute-done((f32[3,1,512]{2,1,0:T(1,128)S(1)}, f32[3,1,512]{2,1,0:T(1,128)S(1)}, u32[]{:S(2)}, u32[]{:S(2)}) %collective-permute-start.25) | collective-permute-done | bytes 6176 | tf_op jit(solution)/shard_map/ppermute | solution.py:24
  294.1 4.4 %collective-permute-done.27 = f32[3,130,1]{2,1,0:T(8,128)S(1)} collective-permute-done((f32[3,130,1]{2,1,0:T(8,128)S(1)}, f32[3,130,1]{2,1,0:T(8,128)S(1)}, u32[]{:S(2)}, u32[]{:S(2)}) %collective-permute-start.27) | collective-permute-done | bytes 1592 | tf_op jit(solution)/shard_map/ppermute | solution.py:24
  304.5 6.0 %multiply_reduce_fusion = (f32[]{:T(128)}, f32[]{:T(128)}, f32[3,128,512]{2,1,0:T(8,128)}) fusion(f32[3,128,512]{2,1,0:T(8,128)S(1)} %get-tuple-element.159, f32[3,128,512]{2,1,0:T(8,128)S(1)} %get-tuple-element.160, f32[3,128,512]{2,1,0:T(8,128)S(1)} %copy-done.5, f32[3,130,1]{2,1,0:T(8,128)S(1)} %collective-permute-done.27, ...), kind=kLoop, calls=%fused_computation.177 | loop fusion | flops 11010046 | bytes 6070408 | tf_op jit(solution)/shard_map/reduce_sum | solution.py:61
  310.5 39.9 %all-reduce.1 = (f32[]{:T(128)}, f32[]{:T(128)}) all-reduce(f32[]{:T(128)} %get-tuple-element.137, f32[]{:T(128)} %get-tuple-element.136), channel_id=1, replica_groups=mesh['gx'=4,'gy'=4,'layer'=2] {'gx','gy','layer'}, use_global_device_ids=true, to_apply=%region_11.12 | all-reduce | flops 2 | bytes 16 | tf_op jit(solution)/shard_map/psum | solution.py:61
  354.2 4.2 %multiply_subtract_fusion = (f32[3,128,512]{2,1,0:T(8,128)}, f32[3,128,512]{2,1,0:T(8,128)}) fusion(f32[3,128,512]{2,1,0:T(8,128)} %copy-done.8, f32[3,128,512]{2,1,0:T(8,128)} %get-tuple-element.158, f32[]{:T(128)S(6)} %div.84, f32[]{:T(128)S(6)} %div.86, f32[3,128,512]{2,1,0:T(8,128)} %get-tuple-element.161, f32[3,128,512]{2,1,0:T(8,128)} %get-tuple-element.164, ...), kind=kLoop, calls=%fused_computation.175 | loop fusion | flops 3145728 | bytes 7864340 | tf_op jit(solution)/shard_map/sub | solution.py:74
  (117 shorter events, 79.1 us)
Async XLA Ops:
  1.5 34.1 %collective-permute-start.2 = (f32[3,1,512]{2,1,0:T(1,128)S(1)}, f32[3,1,512]{2,1,0:T(1,128)S(1)}, u32[]{:S(2)}, u32[]{:S(2)}) collective-permute-start(f32[3,1,512]{2,1,0:T(1,128)S(1)} %get-tuple-element.200), channel_id=1, source_target_pairs={{0,8},{8,16},{16,24},{1,9},{9,17},{17,25},{2,10},{10,18},{18,26},{... | collective-permute-start | bytes 18440 | tf_op jit(solution)/shard_map/ppermute | solution.py:23
  6.3 29.2 %collective-permute-start.1 = (f32[3,1,512]{2,1,0:T(1,128)S(1)}, f32[3,1,512]{2,1,0:T(1,128)S(1)}, u32[]{:S(2)}, u32[]{:S(2)}) collective-permute-start(f32[3,1,512]{2,1,0:T(1,128)S(1)} %get-tuple-element.201), channel_id=1, source_target_pairs={{8,0},{16,8},{24,16},{9,1},{17,9},{25,17},{10,2},{18,10},{26,18},{... | collective-permute-start | bytes 18440 | tf_op jit(solution)/shard_map/ppermute | solution.py:24
  8.5 51.1 %collective-permute-start.8 = (f32[3,1,512]{2,1,0:T(1,128)S(1)}, f32[3,1,512]{2,1,0:T(1,128)S(1)}, u32[]{:S(2)}, u32[]{:S(2)}) collective-permute-start(f32[3,1,512]{2,1,0:T(1,128)S(1)} %get-tuple-element.198), channel_id=1, source_target_pairs={{0,8},{8,16},{16,24},{1,9},{9,17},{17,25},{2,10},{10,18},{18,26},{... | collective-permute-start | bytes 18440 | tf_op jit(solution)/shard_map/ppermute | solution.py:23
  13.0 46.6 %collective-permute-start.7 = (f32[3,1,512]{2,1,0:T(1,128)S(1)}, f32[3,1,512]{2,1,0:T(1,128)S(1)}, u32[]{:S(2)}, u32[]{:S(2)}) collective-permute-start(f32[3,1,512]{2,1,0:T(1,128)S(1)} %get-tuple-element.199), channel_id=1, source_target_pairs={{8,0},{16,8},{24,16},{9,1},{17,9},{25,17},{10,2},{18,10},{26,18},{... | collective-permute-start | bytes 18440 | tf_op jit(solution)/shard_map/ppermute | solution.py:24
  34.2 79.8 %collective-permute-start = (f32[128,512]{1,0:T(8,128)S(1)}, f32[128,512]{1,0:T(8,128)S(1)}, u32[]{:S(2)}, u32[]{:S(2)}) collective-permute-start(f32[128,512]{1,0:T(8,128)S(1)} %get-tuple-element.121), channel_id=1, source_target_pairs={{1,0},{3,2},{5,4},{7,6},{9,8},{11,10},{13,12},{15,14},{17,16},{19,... | collective-permute-start | bytes 786440 | tf_op jit(solution)/shard_map/ppermute | solution.py:13
  35.7 46.5 %collective-permute-start.4 = (f32[3,130,1]{2,1,0:T(8,128)S(1)}, f32[3,130,1]{2,1,0:T(8,128)S(1)}, u32[]{:S(2)}, u32[]{:S(2)}) collective-permute-start(f32[3,130,1]{2,1,0:T(8,128)S(1)} %get-tuple-element.190), channel_id=1, source_target_pairs={{0,2},{2,4},{4,6},{1,3},{3,5},{5,7},{8,10},{10,12},{12,14},{9,11},... | collective-permute-start | bytes 4688 | tf_op jit(solution)/shard_map/ppermute | solution.py:23
  58.3 26.3 %collective-permute-start.3 = (f32[3,130,1]{2,1,0:T(8,128)S(1)}, f32[3,130,1]{2,1,0:T(8,128)S(1)}, u32[]{:S(2)}, u32[]{:S(2)}) collective-permute-start(f32[3,130,1]{2,1,0:T(8,128)S(1)} %get-tuple-element.191), channel_id=1, source_target_pairs={{2,0},{4,2},{6,4},{3,1},{5,3},{7,5},{10,8},{12,10},{14,12},{11,9},... | collective-permute-start | bytes 4688 | tf_op jit(solution)/shard_map/ppermute | solution.py:24
  59.8 28.5 %collective-permute-start.10 = (f32[3,130,1]{2,1,0:T(8,128)S(1)}, f32[3,130,1]{2,1,0:T(8,128)S(1)}, u32[]{:S(2)}, u32[]{:S(2)}) collective-permute-start(f32[3,130,1]{2,1,0:T(8,128)S(1)} %get-tuple-element.188), channel_id=1, source_target_pairs={{0,2},{2,4},{4,6},{1,3},{3,5},{5,7},{8,10},{10,12},{12,14},{9,11},... | collective-permute-start | bytes 4688 | tf_op jit(solution)/shard_map/ppermute | solution.py:23
  80.9 28.5 %collective-permute-start.9 = (f32[3,130,1]{2,1,0:T(8,128)S(1)}, f32[3,130,1]{2,1,0:T(8,128)S(1)}, u32[]{:S(2)}, u32[]{:S(2)}) collective-permute-start(f32[3,130,1]{2,1,0:T(8,128)S(1)} %get-tuple-element.189), channel_id=1, source_target_pairs={{2,0},{4,2},{6,4},{3,1},{5,3},{7,5},{10,8},{12,10},{14,12},{11,9},... | collective-permute-start | bytes 4688 | tf_op jit(solution)/shard_map/ppermute | solution.py:24
  84.9 29.2 %collective-permute-start.6 = (f32[1,130,514]{2,1,0:T(8,128)S(1)}, f32[1,130,514]{2,1,0:T(8,128)S(1)}, u32[]{:S(2)}, u32[]{:S(2)}) collective-permute-start(f32[1,130,514]{2,1,0:T(8,128)S(1)} %get-tuple-element.180), channel_id=1, source_target_pairs={{0,1},{2,3},{4,5},{6,7},{8,9},{10,11},{12,13},{14,15},{16,17},{18,... | collective-permute-start | bytes 801848 | tf_op jit(solution)/shard_map/ppermute | solution.py:23
  87.0 27.1 %collective-permute-start.5 = (f32[1,130,514]{2,1,0:T(8,128)S(1)}, f32[1,130,514]{2,1,0:T(8,128)S(1)}, u32[]{:S(2)}, u32[]{:S(2)}) collective-permute-start(f32[1,130,514]{2,1,0:T(8,128)S(1)} %get-tuple-element.181), channel_id=1, source_target_pairs={{1,0},{3,2},{5,4},{7,6},{9,8},{11,10},{13,12},{15,14},{17,16},{19,... | collective-permute-start | bytes 801848 | tf_op jit(solution)/shard_map/ppermute | solution.py:24
  109.7 8.1 %collective-permute-start.11 = (f32[1,130,514]{2,1,0:T(8,128)S(1)}, f32[1,130,514]{2,1,0:T(8,128)S(1)}, u32[]{:S(2)}, u32[]{:S(2)}) collective-permute-start(f32[1,130,514]{2,1,0:T(8,128)S(1)} %get-tuple-element.178), channel_id=1, source_target_pairs={{1,0},{3,2},{5,4},{7,6},{9,8},{11,10},{13,12},{15,14},{17,16},{19,... | collective-permute-start | bytes 801848 | tf_op jit(solution)/shard_map/ppermute | solution.py:24
  111.0 6.8 %collective-permute-start.12 = (f32[1,130,514]{2,1,0:T(8,128)S(1)}, f32[1,130,514]{2,1,0:T(8,128)S(1)}, u32[]{:S(2)}, u32[]{:S(2)}) collective-permute-start(f32[1,130,514]{2,1,0:T(8,128)S(1)} %get-tuple-element.179), channel_id=1, source_target_pairs={{0,1},{2,3},{4,5},{6,7},{8,9},{10,11},{12,13},{14,15},{16,17},{18,... | collective-permute-start | bytes 801848 | tf_op jit(solution)/shard_map/ppermute | solution.py:23
  122.8 10.1 %collective-permute-start.13 = (f32[3,1,512]{2,1,0:T(1,128)S(1)}, f32[3,1,512]{2,1,0:T(1,128)S(1)}, u32[]{:S(2)}, u32[]{:S(2)}) collective-permute-start(f32[3,1,512]{2,1,0:T(1,128)S(1)} %get-tuple-element.197), channel_id=1, source_target_pairs={{8,0},{16,8},{24,16},{9,1},{17,9},{25,17},{10,2},{18,10},{26,18},{... | collective-permute-start | bytes 18440 | tf_op jit(solution)/shard_map/ppermute | solution.py:24
  133.1 7.6 %collective-permute-start.16 = (f32[3,130,1]{2,1,0:T(8,128)S(1)}, f32[3,130,1]{2,1,0:T(8,128)S(1)}, u32[]{:S(2)}, u32[]{:S(2)}) collective-permute-start(f32[3,130,1]{2,1,0:T(8,128)S(1)} %get-tuple-element.186), channel_id=1, source_target_pairs={{0,2},{2,4},{4,6},{1,3},{3,5},{5,7},{8,10},{10,12},{12,14},{9,11},... | collective-permute-start | bytes 4688 | tf_op jit(solution)/shard_map/ppermute | solution.py:23
  136.7 8.0 %collective-permute-start.15 = (f32[3,130,1]{2,1,0:T(8,128)S(1)}, f32[3,130,1]{2,1,0:T(8,128)S(1)}, u32[]{:S(2)}, u32[]{:S(2)}) collective-permute-start(f32[3,130,1]{2,1,0:T(8,128)S(1)} %get-tuple-element.187), channel_id=1, source_target_pairs={{2,0},{4,2},{6,4},{3,1},{5,3},{7,5},{10,8},{12,10},{14,12},{11,9},... | collective-permute-start | bytes 4688 | tf_op jit(solution)/shard_map/ppermute | solution.py:24
  199.3 5.5 %collective-permute-start.20 = (f32[3,1,512]{2,1,0:T(1,128)S(1)}, f32[3,1,512]{2,1,0:T(1,128)S(1)}, u32[]{:S(2)}, u32[]{:S(2)}) collective-permute-start(f32[3,1,512]{2,1,0:T(1,128)S(1)} %get-tuple-element.194), channel_id=1, source_target_pairs={{0,8},{8,16},{16,24},{1,9},{9,17},{17,25},{2,10},{10,18},{18,26},{... | collective-permute-start | bytes 18440 | tf_op jit(solution)/shard_map/ppermute | solution.py:23
  203.5 5.5 %collective-permute-start.19 = (f32[3,1,512]{2,1,0:T(1,128)S(1)}, f32[3,1,512]{2,1,0:T(1,128)S(1)}, u32[]{:S(2)}, u32[]{:S(2)}) collective-permute-start(f32[3,1,512]{2,1,0:T(1,128)S(1)} %get-tuple-element.195), channel_id=1, source_target_pairs={{8,0},{16,8},{24,16},{9,1},{17,9},{25,17},{10,2},{18,10},{26,18},{... | collective-permute-start | bytes 18440 | tf_op jit(solution)/shard_map/ppermute | solution.py:24
  209.2 5.5 %collective-permute-start.22 = (f32[3,130,1]{2,1,0:T(8,128)S(1)}, f32[3,130,1]{2,1,0:T(8,128)S(1)}, u32[]{:S(2)}, u32[]{:S(2)}) collective-permute-start(f32[3,130,1]{2,1,0:T(8,128)S(1)} %get-tuple-element.184), channel_id=1, source_target_pairs={{0,2},{2,4},{4,6},{1,3},{3,5},{5,7},{8,10},{10,12},{12,14},{9,11},... | collective-permute-start | bytes 4688 | tf_op jit(solution)/shard_map/ppermute | solution.py:23
  211.4 7.7 %collective-permute-start.21 = (f32[3,130,1]{2,1,0:T(8,128)S(1)}, f32[3,130,1]{2,1,0:T(8,128)S(1)}, u32[]{:S(2)}, u32[]{:S(2)}) collective-permute-start(f32[3,130,1]{2,1,0:T(8,128)S(1)} %get-tuple-element.185), channel_id=1, source_target_pairs={{2,0},{4,2},{6,4},{3,1},{5,3},{7,5},{10,8},{12,10},{14,12},{11,9},... | collective-permute-start | bytes 4688 | tf_op jit(solution)/shard_map/ppermute | solution.py:24
  278.0 5.5 %collective-permute-start.26 = (f32[3,1,512]{2,1,0:T(1,128)S(1)}, f32[3,1,512]{2,1,0:T(1,128)S(1)}, u32[]{:S(2)}, u32[]{:S(2)}) collective-permute-start(f32[3,1,512]{2,1,0:T(1,128)S(1)} %get-tuple-element.192), channel_id=1, source_target_pairs={{0,8},{8,16},{16,24},{1,9},{9,17},{17,25},{2,10},{10,18},{18,26},{... | collective-permute-start | bytes 18440 | tf_op jit(solution)/shard_map/ppermute | solution.py:23
  282.2 5.5 %collective-permute-start.25 = (f32[3,1,512]{2,1,0:T(1,128)S(1)}, f32[3,1,512]{2,1,0:T(1,128)S(1)}, u32[]{:S(2)}, u32[]{:S(2)}) collective-permute-start(f32[3,1,512]{2,1,0:T(1,128)S(1)} %get-tuple-element.193), channel_id=1, source_target_pairs={{8,0},{16,8},{24,16},{9,1},{17,9},{25,17},{10,2},{18,10},{26,18},{... | collective-permute-start | bytes 18440 | tf_op jit(solution)/shard_map/ppermute | solution.py:24
  287.9 6.3 %collective-permute-start.28 = (f32[3,130,1]{2,1,0:T(8,128)S(1)}, f32[3,130,1]{2,1,0:T(8,128)S(1)}, u32[]{:S(2)}, u32[]{:S(2)}) collective-permute-start(f32[3,130,1]{2,1,0:T(8,128)S(1)} %get-tuple-element.182), channel_id=1, source_target_pairs={{0,2},{2,4},{4,6},{1,3},{3,5},{5,7},{8,10},{10,12},{12,14},{9,11},... | collective-permute-start | bytes 4688 | tf_op jit(solution)/shard_map/ppermute | solution.py:23
  290.9 7.7 %collective-permute-start.27 = (f32[3,130,1]{2,1,0:T(8,128)S(1)}, f32[3,130,1]{2,1,0:T(8,128)S(1)}, u32[]{:S(2)}, u32[]{:S(2)}) collective-permute-start(f32[3,130,1]{2,1,0:T(8,128)S(1)} %get-tuple-element.183), channel_id=1, source_target_pairs={{2,0},{4,2},{6,4},{3,1},{5,3},{7,5},{10,8},{12,10},{14,12},{11,9},... | collective-permute-start | bytes 4688 | tf_op jit(solution)/shard_map/ppermute | solution.py:24
  (18 other events, 417.6 us)
where the time goes:
time: 361 us; the launch traced here: 358 us
  blocking collectives  120 us (33%)
  starting transfers between devices  107 us (30%)
  waiting for transfers between devices  64 us (18%)
  other arithmetic  39.6 us (11%)
  matrix products  13.2 us (4%)
  between operations  11.5 us (3%)
    psum x3, blocking collectives, both_sums(): lax.psum((jnp.sum(residual * scaled), jnp.sum(scaled * image)), ('gx', 'g...  120 us
    ppermute x15, starting transfers between devices, with_halo(): before = lax.ppermute(last, axis, up)  85.9 us
    ppermute x15, waiting for transfers between devices, with_halo(): after = lax.ppermute(first, axis, down)  53.6 us
    ppermute x15, starting transfers between devices, with_halo(): after = lax.ppermute(first, axis, down)  19.6 us
    reduce_sum x3, other arithmetic, both_sums(): jnp.sum(scaled * image)  17.3 us
    ppermute x15, waiting for transfers between devices, with_halo(): before = lax.ppermute(last, axis, up)  10.4 us
    div x3, other arithmetic, solve(): scaled = residual / diagonal  7.49 us
  transfers between devices with their start and end apart: 31, of which 14 were waited for; matrix products, arithmetic and copies ran while one was open for 7% of the time, Pallas kernels for 0%

commit v1 on v0

--- a/solution.py
+++ b/solution.py
@@ -5,6 +5,11 @@
 
 BLOCK = 512
 ITERS = 3
+
+
+def axis_by_axis(value_2, leading, second):
+    half = lax.psum(value_2, leading)
+    return lax.psum(half, second)
 
 
 def from_behind(value, axis, steps):
@@ -58,7 +63,9 @@
 
 
 def both_sums(residual, scaled, image):
-    return lax.psum((jnp.sum(residual * scaled), jnp.sum(scaled * image)), ("gx", "gy", "layer"))
+    return axis_by_axis(
+        (jnp.sum(residual * scaled), jnp.sum(scaled * image)), "gx", ("gy", "layer")
+    )
 
 
 def solve(apply, diagonal, rhs, start):

time: 361 us -> 312 us (0.86)
  blocking collectives: 120 us -> 75.3 us
  starting transfers between devices: 107 us -> 99.1 us
    psum x3 -> x6, blocking collectives: 120 us -> 75.3 us  [the longest x3 42.7 us: axis_by_axis(): return lax.psum(half, second)]
    ppermute x15, starting transfers between devices: 85.9 us -> 78.4 us  [with_halo(): before = lax.ppermute(last, axis, up)]
  transfers between devices with their start and end apart: 31 -> 31, of which waited for: 14 -> 14; matrix products, arithmetic and copies ran while one was open for 7% -> 8% of each run, Pallas kernels for 0% -> 0%
where the time goes in v1:
time: 312 us; the launch traced here: 310 us
  starting transfers between devices  99.1 us (32%)
  blocking collectives  75.3 us (24%)
  waiting for transfers between devices  66.1 us (21%)
  other arithmetic  41.7 us (13%)
  matrix products  13.2 us (4%)
  between operations  11.1 us (4%)
    ppermute x15, starting transfers between devices, with_halo(): before = lax.ppermute(last, axis, up)  78.4 us
    ppermute x15, waiting for transfers between devices, with_halo(): after = lax.ppermute(first, axis, down)  55.4 us
    psum x3, blocking collectives, axis_by_axis(): return lax.psum(half, second)  42.7 us
    psum x3, blocking collectives, axis_by_axis(): half = lax.psum(value_2, leading)  32.5 us
    ppermute x15, starting transfers between devices, with_halo(): after = lax.ppermute(first, axis, down)  19.4 us
    reduce_sum x3, other arithmetic, both_sums(): jnp.sum(scaled * image)  17.2 us
    ppermute x15, waiting for transfers between devices, with_halo(): before = lax.ppermute(last, axis, up)  10.8 us
    div x3, other arithmetic, solve(): scaled = residual / diagonal  9.78 us
  transfers between devices with their start and end apart: 31, of which 14 were waited for; matrix products, arithmetic and copies ran while one was open for 8% of the time, Pallas kernels for 0%

profile of v1, /device:TPU:0, one launch (start us, length us, event | category | flops | bytes accessed | tf_op | source)
XLA Modules:
  0.0 309.7 jit_solution(3017599682625259105)
XLA Ops:
  1.5 4.9 %collective-permute-start.2 = (f32[3,1,512]{2,1,0:T(1,128)S(1)}, f32[3,1,512]{2,1,0:T(1,128)S(1)}, u32[]{:S(2)}, u32[]{:S(2)}) collective-permute-start(f32[3,1,512]{2,1,0:T(1,128)S(1)} %get-tuple-element.206), channel_id=1, source_target_pairs={{0,8},{8,16},{16,24},{1,9},{9,17},{17,25},{2,10},{10,18},{18,26},{... | collective-permute-start | bytes 18440 | tf_op jit(solution)/shard_map/ppermute | solution.py:28
  8.5 4.5 %collective-permute-start.8 = (f32[3,1,512]{2,1,0:T(1,128)S(1)}, f32[3,1,512]{2,1,0:T(1,128)S(1)}, u32[]{:S(2)}, u32[]{:S(2)}) collective-permute-start(f32[3,1,512]{2,1,0:T(1,128)S(1)} %get-tuple-element.204), channel_id=1, source_target_pairs={{0,8},{8,16},{16,24},{1,9},{9,17},{17,25},{2,10},{10,18},{18,26},{... | collective-permute-start | bytes 18440 | tf_op jit(solution)/shard_map/ppermute | solution.py:28
  15.7 5.8 %fusion.19 = f32[1,16384]{1,0:T(1,128)S(1)} fusion(bf16[256,1]{0,1:T(2,128)(2,1)S(1)} %reshape.111, bf16[1,1,16384,256]{3,2,1,0:T(8,128)(2,1)} %param.14), kind=kOutput, calls=%fused_computation.28 | convolution fusion | flops 8388608 | bytes 8454656 | tf_op jit(solution)/shard_map/dot_general | solution.py:96
  21.5 12.7 %while.15 = (s32[]{:T(128)}, f32[128,512]{1,0:T(8,128)S(1)}, s32[]{:T(128)}, s32[16384]{0:T(1024)}, f32[16384]{0:T(1024)S(1)}, /*index=5*/s32[]{:T(128)}, s32[]{:T(128)}, s32[]{:T(128)}, s32[]{:T(128)}) while((s32[]{:T(128)}, f32[128,512]{1,0:T(8,128)S(1)}, s32[]{:T(128)}, s32[16384]{0:T(1024)}, f32[16384]{0:T(1024)S(1)}, ...), condition=%wide.region_1.2_spmd.clone, body=%wide.region_0.1_spmd.clone.sunk | while | flops 135407104 | bytes 1071251 | solution.py:121
  35.7 22.6 %collective-permute-start.4 = (f32[3,130,1]{2,1,0:T(8,128)S(1)}, f32[3,130,1]{2,1,0:T(8,128)S(1)}, u32[]{:S(2)}, u32[]{:S(2)}) collective-permute-start(f32[3,130,1]{2,1,0:T(8,128)S(1)} %get-tuple-element.196), channel_id=1, source_target_pairs={{0,2},{2,4},{4,6},{1,3},{3,5},{5,7},{8,10},{10,12},{12,14},{9,11},... | collective-permute-start | bytes 4688 | tf_op jit(solution)/shard_map/ppermute | solution.py:28
  59.8 21.1 %collective-permute-start.10 = (f32[3,130,1]{2,1,0:T(8,128)S(1)}, f32[3,130,1]{2,1,0:T(8,128)S(1)}, u32[]{:S(2)}, u32[]{:S(2)}) collective-permute-start(f32[3,130,1]{2,1,0:T(8,128)S(1)} %get-tuple-element.194), channel_id=1, source_target_pairs={{0,2},{2,4},{4,6},{1,3},{3,5},{5,7},{8,10},{10,12},{12,14},{9,11},... | collective-permute-start | bytes 4688 | tf_op jit(solution)/shard_map/ppermute | solution.py:28
  88.3 21.1 %collective-permute-done.9 = f32[3,130,1]{2,1,0:T(8,128)S(1)} collective-permute-done((f32[3,130,1]{2,1,0:T(8,128)S(1)}, f32[3,130,1]{2,1,0:T(8,128)S(1)}, u32[]{:S(2)}, u32[]{:S(2)}) %collective-permute-start.9) | collective-permute-done | bytes 1592 | tf_op jit(solution)/shard_map/ppermute | solution.py:29
  117.8 6.0 %fusion.83 = (f32[3,128,512]{2,1,0:T(8,128)S(1)}, f32[3,128,512]{2,1,0:T(8,128)S(1)}) fusion(f32[3,128,512]{2,1,0:T(8,128)S(1)} %fusion.76, f32[3,128,512]{2,1,0:T(8,128)S(1)} %get-tuple-element.175, f32[3,130,1]{2,1,0:T(8,128)S(1)} %collective-permute-done.9, f32[3,1,512]{2,1,0:T(1,128)S(1)} %collective-permute-done.7, f32[3,128,512]{2,1,0:T(8,128)} %param.21, ...), kind=kLoop, calls=%fused_computation.238 | loop fusion | flops 10616832 | bytes 6332544 | tf_op jit(solution)/shard_map/div | solution.py:74
  126.4 8.7 %collective-permute-done.13 = f32[3,1,512]{2,1,0:T(1,128)S(1)} collective-permute-done((f32[3,1,512]{2,1,0:T(1,128)S(1)}, f32[3,1,512]{2,1,0:T(1,128)S(1)}, u32[]{:S(2)}, u32[]{:S(2)}) %collective-permute-start.13) | collective-permute-done | bytes 6176 | tf_op jit(solution)/shard_map/ppermute | solution.py:29
  142.9 4.1 %collective-permute-done.15 = f32[3,130,1]{2,1,0:T(8,128)S(1)} collective-permute-done((f32[3,130,1]{2,1,0:T(8,128)S(1)}, f32[3,130,1]{2,1,0:T(8,128)S(1)}, u32[]{:S(2)}, u32[]{:S(2)}) %collective-permute-start.15) | collective-permute-done | bytes 1592 | tf_op jit(solution)/shard_map/ppermute | solution.py:29
  153.0 5.0 %multiply_reduce_fusion.4 = (f32[]{:T(128)}, f32[]{:T(128)}, f32[3,128,512]{2,1,0:T(8,128)}) fusion(f32[3,128,512]{2,1,0:T(8,128)S(1)} %get-tuple-element.171, f32[3,128,512]{2,1,0:T(8,128)S(1)} %get-tuple-element.172, f32[3,128,512]{2,1,0:T(8,128)S(1)} %get-tuple-element.175, f32[3,130,1]{2,1,0:T(8,128)S(1)} %collective-permute-done.15, ...), kind=kLoop, calls=%fused_computation.184 | loop fusion | flops 11010046 | bytes 6070408 | tf_op jit(solution)/shard_map/reduce_sum | solution.py:67
  158.0 10.6 %all-reduce.6 = (f32[]{:T(128)}, f32[]{:T(128)}) all-reduce(f32[]{:T(128)} %get-tuple-element.141, f32[]{:T(128)} %get-tuple-element.140), channel_id=1, replica_groups=mesh['gx'=4,'gy'=4,'layer'=2] {'gx'}, use_global_device_ids=true, to_apply=%region_3.4 | all-reduce | flops 2 | bytes 16 | tf_op jit(solution)/shard_map/psum | solution.py:11
  168.6 14.2 %all-reduce.3 = (f32[]{:T(128)}, f32[]{:T(128)}) all-reduce(f32[]{:T(128)} %get-tuple-element.162, f32[]{:T(128)} %get-tuple-element.163), channel_id=1, replica_groups=mesh['gx'=4,'gy'=4,'layer'=2] {'gy','layer'}, use_global_device_ids=true, to_apply=%region_4.5 | all-reduce | flops 2 | bytes 16 | tf_op jit(solution)/shard_map/psum | solution.py:12
  188.7 5.4 %collective-permute-done.19 = f32[3,1,512]{2,1,0:T(1,128)S(1)} collective-permute-done((f32[3,1,512]{2,1,0:T(1,128)S(1)}, f32[3,1,512]{2,1,0:T(1,128)S(1)}, u32[]{:S(2)}, u32[]{:S(2)}) %collective-permute-start.19) | collective-permute-done | bytes 6176 | tf_op jit(solution)/shard_map/ppermute | solution.py:29
  199.1 4.1 %collective-permute-done.21 = f32[3,130,1]{2,1,0:T(8,128)S(1)} collective-permute-done((f32[3,130,1]{2,1,0:T(8,128)S(1)}, f32[3,130,1]{2,1,0:T(8,128)S(1)}, u32[]{:S(2)}, u32[]{:S(2)}) %collective-permute-start.21) | collective-permute-done | bytes 1592 | tf_op jit(solution)/shard_map/ppermute | solution.py:29
  209.2 6.3 %multiply_reduce_fusion.2 = (f32[]{:T(128)}, f32[]{:T(128)}, f32[3,128,512]{2,1,0:T(8,128)}) fusion(f32[3,128,512]{2,1,0:T(8,128)S(1)} %get-tuple-element.168, f32[3,128,512]{2,1,0:T(8,128)S(1)} %get-tuple-element.169, f32[3,128,512]{2,1,0:T(8,128)} %copy-done.4, f32[3,130,1]{2,1,0:T(8,128)S(1)} %collective-permute-done.21, ...), kind=kLoop, calls=%fused_computation.181 | loop fusion | flops 11010046 | bytes 6070408 | tf_op jit(solution)/shard_map/reduce_sum | solution.py:67
  215.5 11.0 %all-reduce.5 = (f32[]{:T(128)}, f32[]{:T(128)}) all-reduce(f32[]{:T(128)} %get-tuple-element.139, f32[]{:T(128)} %get-tuple-element.138), channel_id=1, replica_groups=mesh['gx'=4,'gy'=4,'layer'=2] {'gx'}, use_global_device_ids=true, to_apply=%region_9.10 | all-reduce | flops 2 | bytes 16 | tf_op jit(solution)/shard_map/psum | solution.py:11
  226.5 14.2 %all-reduce.2 = (f32[]{:T(128)}, f32[]{:T(128)}) all-reduce(f32[]{:T(128)} %get-tuple-element.160, f32[]{:T(128)} %get-tuple-element.161), channel_id=1, replica_groups=mesh['gx'=4,'gy'=4,'layer'=2] {'gy','layer'}, use_global_device_ids=true, to_apply=%region_10.11 | all-reduce | flops 2 | bytes 16 | tf_op jit(solution)/shard_map/psum | solution.py:12
  250.1 5.4 %collective-permute-done.25 = f32[3,1,512]{2,1,0:T(1,128)S(1)} collective-permute-done((f32[3,1,512]{2,1,0:T(1,128)S(1)}, f32[3,1,512]{2,1,0:T(1,128)S(1)}, u32[]{:S(2)}, u32[]{:S(2)}) %collective-permute-start.25) | collective-permute-done | bytes 6176 | tf_op jit(solution)/shard_map/ppermute | solution.py:29
  260.4 4.1 %collective-permute-done.27 = f32[3,130,1]{2,1,0:T(8,128)S(1)} collective-permute-done((f32[3,130,1]{2,1,0:T(8,128)S(1)}, f32[3,130,1]{2,1,0:T(8,128)S(1)}, u32[]{:S(2)}, u32[]{:S(2)}) %collective-permute-start.27) | collective-permute-done | bytes 1592 | tf_op jit(solution)/shard_map/ppermute | solution.py:29
  270.5 6.0 %multiply_reduce_fusion = (f32[]{:T(128)}, f32[]{:T(128)}, f32[3,128,512]{2,1,0:T(8,128)}) fusion(f32[3,128,512]{2,1,0:T(8,128)S(1)} %get-tuple-element.165, f32[3,128,512]{2,1,0:T(8,128)S(1)} %get-tuple-element.166, f32[3,128,512]{2,1,0:T(8,128)S(1)} %copy-done.5, f32[3,130,1]{2,1,0:T(8,128)S(1)} %collective-permute-done.27, ...), kind=kLoop, calls=%fused_computation.177 | loop fusion | flops 11010046 | bytes 6070408 | tf_op jit(solution)/shard_map/reduce_sum | solution.py:67
  276.5 10.9 %all-reduce.4 = (f32[]{:T(128)}, f32[]{:T(128)}) all-reduce(f32[]{:T(128)} %get-tuple-element.137, f32[]{:T(128)} %get-tuple-element.136), channel_id=1, replica_groups=mesh['gx'=4,'gy'=4,'layer'=2] {'gx'}, use_global_device_ids=true, to_apply=%region_15.16 | all-reduce | flops 2 | bytes 16 | tf_op jit(solution)/shard_map/psum | solution.py:11
  287.4 14.3 %all-reduce.1 = (f32[]{:T(128)}, f32[]{:T(128)}) all-reduce(f32[]{:T(128)} %get-tuple-element.158, f32[]{:T(128)} %get-tuple-element.159), channel_id=1, replica_groups=mesh['gx'=4,'gy'=4,'layer'=2] {'gy','layer'}, use_global_device_ids=true, to_apply=%region_16.17 | all-reduce | flops 2 | bytes 16 | tf_op jit(solution)/shard_map/psum | solution.py:12
  305.4 4.2 %multiply_subtract_fusion = (f32[3,128,512]{2,1,0:T(8,128)}, f32[3,128,512]{2,1,0:T(8,128)}) fusion(f32[3,128,512]{2,1,0:T(8,128)} %copy-done.8, f32[3,128,512]{2,1,0:T(8,128)} %get-tuple-element.164, f32[]{:T(128)S(6)} %div.84, f32[]{:T(128)S(6)} %div.86, f32[3,128,512]{2,1,0:T(8,128)} %get-tuple-element.167, f32[3,128,512]{2,1,0:T(8,128)} %get-tuple-element.170, ...), kind=kLoop, calls=%fused_computation.175 | loop fusion | flops 3145728 | bytes 7864340 | tf_op jit(solution)/shard_map/sub | solution.py:81
  (120 shorter events, 83.9 us)
Async XLA Ops:
  1.5 34.1 %collective-permute-start.2 = (f32[3,1,512]{2,1,0:T(1,128)S(1)}, f32[3,1,512]{2,1,0:T(1,128)S(1)}, u32[]{:S(2)}, u32[]{:S(2)}) collective-permute-start(f32[3,1,512]{2,1,0:T(1,128)S(1)} %get-tuple-element.206), channel_id=1, source_target_pairs={{0,8},{8,16},{16,24},{1,9},{9,17},{17,25},{2,10},{10,18},{18,26},{... | collective-permute-start | bytes 18440 | tf_op jit(solution)/shard_map/ppermute | solution.py:28
  6.3 29.2 %collective-permute-start.1 = (f32[3,1,512]{2,1,0:T(1,128)S(1)}, f32[3,1,512]{2,1,0:T(1,128)S(1)}, u32[]{:S(2)}, u32[]{:S(2)}) collective-permute-start(f32[3,1,512]{2,1,0:T(1,128)S(1)} %get-tuple-element.207), channel_id=1, source_target_pairs={{8,0},{16,8},{24,16},{9,1},{17,9},{25,17},{10,2},{18,10},{26,18},{... | collective-permute-start | bytes 18440 | tf_op jit(solution)/shard_map/ppermute | solution.py:29
  8.5 51.1 %collective-permute-start.8 = (f32[3,1,512]{2,1,0:T(1,128)S(1)}, f32[3,1,512]{2,1,0:T(1,128)S(1)}, u32[]{:S(2)}, u32[]{:S(2)}) collective-permute-start(f32[3,1,512]{2,1,0:T(1,128)S(1)} %get-tuple-element.204), channel_id=1, source_target_pairs={{0,8},{8,16},{16,24},{1,9},{9,17},{17,25},{2,10},{10,18},{18,26},{... | collective-permute-start | bytes 18440 | tf_op jit(solution)/shard_map/ppermute | solution.py:28
  13.0 46.6 %collective-permute-start.7 = (f32[3,1,512]{2,1,0:T(1,128)S(1)}, f32[3,1,512]{2,1,0:T(1,128)S(1)}, u32[]{:S(2)}, u32[]{:S(2)}) collective-permute-start(f32[3,1,512]{2,1,0:T(1,128)S(1)} %get-tuple-element.205), channel_id=1, source_target_pairs={{8,0},{16,8},{24,16},{9,1},{17,9},{25,17},{10,2},{18,10},{26,18},{... | collective-permute-start | bytes 18440 | tf_op jit(solution)/shard_map/ppermute | solution.py:29
  34.2 79.8 %collective-permute-start = (f32[128,512]{1,0:T(8,128)S(1)}, f32[128,512]{1,0:T(8,128)S(1)}, u32[]{:S(2)}, u32[]{:S(2)}) collective-permute-start(f32[128,512]{1,0:T(8,128)S(1)} %get-tuple-element.121), channel_id=1, source_target_pairs={{1,0},{3,2},{5,4},{7,6},{9,8},{11,10},{13,12},{15,14},{17,16},{19,... | collective-permute-start | bytes 786440 | tf_op jit(solution)/shard_map/ppermute | solution.py:18
  35.7 46.5 %collective-permute-start.4 = (f32[3,130,1]{2,1,0:T(8,128)S(1)}, f32[3,130,1]{2,1,0:T(8,128)S(1)}, u32[]{:S(2)}, u32[]{:S(2)}) collective-permute-start(f32[3,130,1]{2,1,0:T(8,128)S(1)} %get-tuple-element.196), channel_id=1, source_target_pairs={{0,2},{2,4},{4,6},{1,3},{3,5},{5,7},{8,10},{10,12},{12,14},{9,11},... | collective-permute-start | bytes 4688 | tf_op jit(solution)/shard_map/ppermute | solution.py:28
  58.3 26.3 %collective-permute-start.3 = (f32[3,130,1]{2,1,0:T(8,128)S(1)}, f32[3,130,1]{2,1,0:T(8,128)S(1)}, u32[]{:S(2)}, u32[]{:S(2)}) collective-permute-start(f32[3,130,1]{2,1,0:T(8,128)S(1)} %get-tuple-element.197), channel_id=1, source_target_pairs={{2,0},{4,2},{6,4},{3,1},{5,3},{7,5},{10,8},{12,10},{14,12},{11,9},... | collective-permute-start | bytes 4688 | tf_op jit(solution)/shard_map/ppermute | solution.py:29
  59.8 28.5 %collective-permute-start.10 = (f32[3,130,1]{2,1,0:T(8,128)S(1)}, f32[3,130,1]{2,1,0:T(8,128)S(1)}, u32[]{:S(2)}, u32[]{:S(2)}) collective-permute-start(f32[3,130,1]{2,1,0:T(8,128)S(1)} %get-tuple-element.194), channel_id=1, source_target_pairs={{0,2},{2,4},{4,6},{1,3},{3,5},{5,7},{8,10},{10,12},{12,14},{9,11},... | collective-permute-start | bytes 4688 | tf_op jit(solution)/shard_map/ppermute | solution.py:28
  80.9 28.5 %collective-permute-start.9 = (f32[3,130,1]{2,1,0:T(8,128)S(1)}, f32[3,130,1]{2,1,0:T(8,128)S(1)}, u32[]{:S(2)}, u32[]{:S(2)}) collective-permute-start(f32[3,130,1]{2,1,0:T(8,128)S(1)} %get-tuple-element.195), channel_id=1, source_target_pairs={{2,0},{4,2},{6,4},{3,1},{5,3},{7,5},{10,8},{12,10},{14,12},{11,9},... | collective-permute-start | bytes 4688 | tf_op jit(solution)/shard_map/ppermute | solution.py:29
  84.9 29.2 %collective-permute-start.6 = (f32[1,130,514]{2,1,0:T(8,128)S(1)}, f32[1,130,514]{2,1,0:T(8,128)S(1)}, u32[]{:S(2)}, u32[]{:S(2)}) collective-permute-start(f32[1,130,514]{2,1,0:T(8,128)S(1)} %get-tuple-element.186), channel_id=1, source_target_pairs={{0,1},{2,3},{4,5},{6,7},{8,9},{10,11},{12,13},{14,15},{16,17},{18,... | collective-permute-start | bytes 801848 | tf_op jit(solution)/shard_map/ppermute | solution.py:28
  87.0 27.1 %collective-permute-start.5 = (f32[1,130,514]{2,1,0:T(8,128)S(1)}, f32[1,130,514]{2,1,0:T(8,128)S(1)}, u32[]{:S(2)}, u32[]{:S(2)}) collective-permute-start(f32[1,130,514]{2,1,0:T(8,128)S(1)} %get-tuple-element.187), channel_id=1, source_target_pairs={{1,0},{3,2},{5,4},{7,6},{9,8},{11,10},{13,12},{15,14},{17,16},{19,... | collective-permute-start | bytes 801848 | tf_op jit(solution)/shard_map/ppermute | solution.py:29
  109.7 8.1 %collective-permute-start.11 = (f32[1,130,514]{2,1,0:T(8,128)S(1)}, f32[1,130,514]{2,1,0:T(8,128)S(1)}, u32[]{:S(2)}, u32[]{:S(2)}) collective-permute-start(f32[1,130,514]{2,1,0:T(8,128)S(1)} %get-tuple-element.184), channel_id=1, source_target_pairs={{1,0},{3,2},{5,4},{7,6},{9,8},{11,10},{13,12},{15,14},{17,16},{19,... | collective-permute-start | bytes 801848 | tf_op jit(solution)/shard_map/ppermute | solution.py:29
  111.0 6.8 %collective-permute-start.12 = (f32[1,130,514]{2,1,0:T(8,128)S(1)}, f32[1,130,514]{2,1,0:T(8,128)S(1)}, u32[]{:S(2)}, u32[]{:S(2)}) collective-permute-start(f32[1,130,514]{2,1,0:T(8,128)S(1)} %get-tuple-element.185), channel_id=1, source_target_pairs={{0,1},{2,3},{4,5},{6,7},{8,9},{10,11},{12,13},{14,15},{16,17},{18,... | collective-permute-start | bytes 801848 | tf_op jit(solution)/shard_map/ppermute | solution.py:28
  125.1 10.1 %collective-permute-start.13 = (f32[3,1,512]{2,1,0:T(1,128)S(1)}, f32[3,1,512]{2,1,0:T(1,128)S(1)}, u32[]{:S(2)}, u32[]{:S(2)}) collective-permute-start(f32[3,1,512]{2,1,0:T(1,128)S(1)} %get-tuple-element.203), channel_id=1, source_target_pairs={{8,0},{16,8},{24,16},{9,1},{17,9},{25,17},{10,2},{18,10},{26,18},{... | collective-permute-start | bytes 18440 | tf_op jit(solution)/shard_map/ppermute | solution.py:29
  135.3 7.6 %collective-permute-start.16 = (f32[3,130,1]{2,1,0:T(8,128)S(1)}, f32[3,130,1]{2,1,0:T(8,128)S(1)}, u32[]{:S(2)}, u32[]{:S(2)}) collective-permute-start(f32[3,130,1]{2,1,0:T(8,128)S(1)} %get-tuple-element.192), channel_id=1, source_target_pairs={{0,2},{2,4},{4,6},{1,3},{3,5},{5,7},{8,10},{10,12},{12,14},{9,11},... | collective-permute-start | bytes 4688 | tf_op jit(solution)/shard_map/ppermute | solution.py:28
  139.0 8.0 %collective-permute-start.15 = (f32[3,130,1]{2,1,0:T(8,128)S(1)}, f32[3,130,1]{2,1,0:T(8,128)S(1)}, u32[]{:S(2)}, u32[]{:S(2)}) collective-permute-start(f32[3,130,1]{2,1,0:T(8,128)S(1)} %get-tuple-element.193), channel_id=1, source_target_pairs={{2,0},{4,2},{6,4},{3,1},{5,3},{7,5},{10,8},{12,10},{14,12},{11,9},... | collective-permute-start | bytes 4688 | tf_op jit(solution)/shard_map/ppermute | solution.py:29
  147.4 4.4 %collective-permute-start.17 = (f32[1,130,514]{2,1,0:T(8,128)S(1)}, f32[1,130,514]{2,1,0:T(8,128)S(1)}, u32[]{:S(2)}, u32[]{:S(2)}) collective-permute-start(f32[1,130,514]{2,1,0:T(8,128)S(1)} %get-tuple-element.182), channel_id=1, source_target_pairs={{1,0},{3,2},{5,4},{7,6},{9,8},{11,10},{13,12},{15,14},{17,16},{19,... | collective-permute-start | bytes 801848 | tf_op jit(solution)/shard_map/ppermute | solution.py:29
  187.4 6.7 %collective-permute-start.19 = (f32[3,1,512]{2,1,0:T(1,128)S(1)}, f32[3,1,512]{2,1,0:T(1,128)S(1)}, u32[]{:S(2)}, u32[]{:S(2)}) collective-permute-start(f32[3,1,512]{2,1,0:T(1,128)S(1)} %get-tuple-element.201), channel_id=1, source_target_pairs={{8,0},{16,8},{24,16},{9,1},{17,9},{25,17},{10,2},{18,10},{26,18},{... | collective-permute-start | bytes 18440 | tf_op jit(solution)/shard_map/ppermute | solution.py:29
  194.2 4.9 %collective-permute-start.22 = (f32[3,130,1]{2,1,0:T(8,128)S(1)}, f32[3,130,1]{2,1,0:T(8,128)S(1)}, u32[]{:S(2)}, u32[]{:S(2)}) collective-permute-start(f32[3,130,1]{2,1,0:T(8,128)S(1)} %get-tuple-element.190), channel_id=1, source_target_pairs={{0,2},{2,4},{4,6},{1,3},{3,5},{5,7},{8,10},{10,12},{12,14},{9,11},... | collective-permute-start | bytes 4688 | tf_op jit(solution)/shard_map/ppermute | solution.py:28
  195.5 7.7 %collective-permute-start.21 = (f32[3,130,1]{2,1,0:T(8,128)S(1)}, f32[3,130,1]{2,1,0:T(8,128)S(1)}, u32[]{:S(2)}, u32[]{:S(2)}) collective-permute-start(f32[3,130,1]{2,1,0:T(8,128)S(1)} %get-tuple-element.191), channel_id=1, source_target_pairs={{2,0},{4,2},{6,4},{3,1},{5,3},{7,5},{10,8},{12,10},{14,12},{11,9},... | collective-permute-start | bytes 4688 | tf_op jit(solution)/shard_map/ppermute | solution.py:29
  203.6 4.6 %collective-permute-start.23 = (f32[1,130,514]{2,1,0:T(8,128)S(1)}, f32[1,130,514]{2,1,0:T(8,128)S(1)}, u32[]{:S(2)}, u32[]{:S(2)}) collective-permute-start(f32[1,130,514]{2,1,0:T(8,128)S(1)} %get-tuple-element.180), channel_id=1, source_target_pairs={{1,0},{3,2},{5,4},{7,6},{9,8},{11,10},{13,12},{15,14},{17,16},{19,... | collective-permute-start | bytes 801848 | tf_op jit(solution)/shard_map/ppermute | solution.py:29
  248.7 6.7 %collective-permute-start.25 = (f32[3,1,512]{2,1,0:T(1,128)S(1)}, f32[3,1,512]{2,1,0:T(1,128)S(1)}, u32[]{:S(2)}, u32[]{:S(2)}) collective-permute-start(f32[3,1,512]{2,1,0:T(1,128)S(1)} %get-tuple-element.199), channel_id=1, source_target_pairs={{8,0},{16,8},{24,16},{9,1},{17,9},{25,17},{10,2},{18,10},{26,18},{... | collective-permute-start | bytes 18440 | tf_op jit(solution)/shard_map/ppermute | solution.py:29
  255.6 4.9 %collective-permute-start.28 = (f32[3,130,1]{2,1,0:T(8,128)S(1)}, f32[3,130,1]{2,1,0:T(8,128)S(1)}, u32[]{:S(2)}, u32[]{:S(2)}) collective-permute-start(f32[3,130,1]{2,1,0:T(8,128)S(1)} %get-tuple-element.188), channel_id=1, source_target_pairs={{0,2},{2,4},{4,6},{1,3},{3,5},{5,7},{8,10},{10,12},{12,14},{9,11},... | collective-permute-start | bytes 4688 | tf_op jit(solution)/shard_map/ppermute | solution.py:28
  256.9 7.7 %collective-permute-start.27 = (f32[3,130,1]{2,1,0:T(8,128)S(1)}, f32[3,130,1]{2,1,0:T(8,128)S(1)}, u32[]{:S(2)}, u32[]{:S(2)}) collective-permute-start(f32[3,130,1]{2,1,0:T(8,128)S(1)} %get-tuple-element.189), channel_id=1, source_target_pairs={{2,0},{4,2},{6,4},{3,1},{5,3},{7,5},{10,8},{12,10},{14,12},{11,9},... | collective-permute-start | bytes 4688 | tf_op jit(solution)/shard_map/ppermute | solution.py:29
  (18 other events, 406.7 us)
